TPU v7x, 32 devices: a whole 2x2x4 slice. The times are simulated.
32 devices in a mesh: design: 2 (over x), blk: 16 (over z, y, core).
Axes of the slice: x: 2, y: 2, z: 4, core: 2. Of those that a mesh axis runs over, the one named last changes fastest.
Arguments:
- right_side: float32 [6, 256, 1024], P(None, ('design', 'blk')), parts along dimension 1, may hold values from -6 to 6
- adjoint_start: float32 [6, 256, 1024], P(None, ('design', 'blk')), parts along dimension 1, may hold values from -3 to 3
- diag_inverse: float32 [6, 6, 256, 1024], P(None, None, ('design', 'blk')), parts along dimension 2
- face_jacobian: bfloat16 [4, 6, 6, 256, 1024], P(None, None, None, ('design', 'blk')), parts along dimension 3, may hold values from -0.25 to 0.25
- receptor_cell: int32 [32, 16, 16], P(('design', 'blk')), parts along dimension 0, may hold values from 0 to 8191
- donor_cell: int32 [32, 16, 4, 16], P(('design', 'blk')), parts along dimension 0, may hold values from 0 to 8191
- donor_weight: float32 [32, 16, 4, 16], P(('design', 'blk')), parts along dimension 0, may hold values from 0 to 1, as said below
- live_count: int32 [32, 16], P(('design', 'blk')), parts along dimension 0, may hold values from 0 to 16, as said below
Outputs:
- adjoint: float32 [6, 256, 1024], P(None, ('design', 'blk')), parts along dimension 1
- correction_norms: float32 [4], P('design'), parts along dimension 0
There are 2 independent parts, one for each index of `design`. A program takes and returns all parts, laid end to end along the dimension named above; each array names one. Nothing has to cross between parts.
Inputs may be any that keep to these rules, and one draw needn't show every extreme that they name: live_count[s, d] counts the leading live slots of list (s, d); in every draw some partition d has 16 live slots from every source s. `donor_weight`: the four weights of each slot are positive and sum to 1.
All inputs are finite; a program needn't handle non-finite values.
Results may differ from a plain program's by a relative error of at most 0.0003.
Values sent between devices are 32-bit elements; how exact they have to be, the bound alone decides.
A program may use at most 64 MiB of HBM per device.

v0:
```python
import math
import jax
import jax.numpy as jnp
from jax import lax
from jax.sharding import PartitionSpec as P

SWEEPS = 2


def padded_2(block, sides, width):
    for axis, dim in sides:
        count = lax.axis_size(axis)
        forward = [(i, i + 1) for i in range(count - 1)]
        backward = [(target, source) for source, target in forward]
        low = lax.ppermute(
            lax.slice_in_dim(block, block.shape[dim] - width, None, axis=dim), axis, forward
        )
        high = lax.ppermute(lax.slice_in_dim(block, 0, width, axis=dim), axis, backward)
        block = jnp.concatenate([low, block, high], axis=dim)
    return block


def group_count(parts, rows_each):
    best = 1
    for count in range(1, parts + 1):
        if parts % count == 0 and count * rows_each <= 2048:
            best = count
    return best


def split_index(index, width, blocks):
    upper = index // width
    lower = index - upper * width
    block_hot = (upper[:, None] == jnp.arange(blocks, dtype=jnp.int32)[None, :]).astype(jnp.float32)
    offset_hot = (lower[:, None] == jnp.arange(width, dtype=jnp.int32)[None, :]).astype(jnp.float32)
    return (block_hot, offset_hot)


def pick_cells(field, index, rows_each):
    nvar, cells = field.shape
    parts = index.shape[0] // rows_each
    width = math.gcd(cells, 128)
    blocks = cells // width
    shaped = field.reshape(nvar, blocks, width)
    members = group_count(parts, rows_each)
    grouped = index.reshape(parts // members, members * rows_each)

    def pick_one_group(rows_index):
        block_hot, offset_hot = split_index(rows_index, width, blocks)
        picked = jnp.einsum("tb,abo->tao", block_hot, shaped, precision=lax.Precision.HIGHEST)
        return jnp.sum(picked * offset_hot[:, None, :], axis=2)

    gathered = lax.map(pick_one_group, grouped)
    return jnp.transpose(gathered, (2, 0, 1)).reshape(nvar, -1)


def spread_cells(terms, index, cells, rows_each):
    nvar = terms.shape[0]
    parts = index.shape[0] // rows_each
    width = math.gcd(cells, 128)
    blocks = cells // width
    members = group_count(parts, rows_each)
    groups = parts // members
    grouped_index = index.reshape(groups, members * rows_each)
    grouped_terms = jnp.transpose(terms.reshape(nvar, groups, members * rows_each), (1, 0, 2))

    def spread_one_group(total, pieces):
        rows_index, rows_terms = pieces
        block_hot, offset_hot = split_index(rows_index, width, blocks)
        weighted = rows_terms[:, :, None] * block_hot[None]
        added = jnp.einsum("atb,to->abo", weighted, offset_hot, precision=lax.Precision.HIGHEST)
        return (total + added, None)

    start = jnp.zeros((nvar, blocks, width), jnp.float32)
    total, unused = lax.scan(spread_one_group, start, (grouped_index, grouped_terms))
    return total.reshape(nvar, cells)


def face_coupling(psi, face_jacobian):
    padded = padded_2(psi, (("blk", 1),), 1)
    widened = jnp.pad(psi, ((0, 0), (0, 0), (1, 1)))
    sides = (padded[:, :-2, :], padded[:, 2:, :], widened[:, :, :-2], widened[:, :, 2:])
    coupled = jnp.zeros(psi.shape, jnp.float32)
    for face in range(4):
        coupled = coupled + jnp.einsum(
            "abij,bij->aij",
            face_jacobian[face].astype(jnp.float32),
            sides[face],
            precision=lax.Precision.HIGHEST,
        )
    return coupled


def body(
    right_side,
    adjoint_start,
    diag_inverse,
    face_jacobian,
    receptor_cell,
    donor_cell,
    donor_weight,
    live_count,
):
    nvar, rows, cols = right_side.shape
    cells = rows * cols
    slots = receptor_cell.shape[2]
    live = (jnp.arange(slots, dtype=jnp.int32)[None, :] < live_count[0][:, None]).astype(
        jnp.float32
    )
    targets = lax.all_to_all(donor_cell[0], "blk", split_axis=0, concat_axis=0, tiled=True).reshape(
        -1
    )
    sources = receptor_cell[0].reshape(-1)
    rhs_local = jnp.sum(right_side * right_side)
    psi = adjoint_start
    partials = []
    for sweep in range(SWEEPS):
        picked = pick_cells(psi.reshape(nvar, cells), sources, slots)
        values = picked.reshape(nvar, -1, slots) * live[None]
        weighted = values[:, :, None, :] * donor_weight[0][None]
        terms = lax.all_to_all(weighted, "blk", split_axis=1, concat_axis=1, tiled=True)
        spread = spread_cells(terms.reshape(nvar, -1), targets, cells, 4 * slots)
        coupled = face_coupling(psi, face_jacobian)
        source = right_side - coupled + spread.reshape(psi.shape)
        new = jnp.einsum("abij,bij->aij", diag_inverse, source, precision=lax.Precision.HIGHEST)
        change = new - psi
        partial_sq = jnp.sum(change * change)
        partials.append(partial_sq)
        psi = new
    totals = lax.psum(jnp.stack([rhs_local] + partials), "blk")
    result_norms = jnp.sqrt(totals[1:] / (totals[0] + 1e-06))
    return (psi, result_norms)


def solution(mesh):
    return jax.shard_map(
        body,
        mesh=mesh,
        in_specs=(
            P(None, ("design", "blk"), None),
            P(None, ("design", "blk"), None),
            P(None, None, ("design", "blk"), None),
            P(None, None, None, ("design", "blk"), None),
            P(("design", "blk"), None, None),
            P(("design", "blk"), None, None, None),
            P(("design", "blk"), None, None, None),
            P(("design", "blk"), None),
        ),
        out_specs=(P(None, ("design", "blk"), None), P("design")),
        check_vma=False,
    )
```

profile of v0, /device:TPU:0, one launch (start us, length us, event | category | flops | bytes accessed | tf_op | source)
XLA Modules:
  0.0 102.9 jit_solution(15937769331518278682)
XLA Ops:
  0.7 7.6 %all-to-all-start.1 = ((s32[16,4,16]{2,1,0:T(4,128)}), s32[16,4,16]{2,1,0:T(4,128)S(1)}, u32[]{:S(2)}, u32[]{:S(2)}) async-start(s32[16,4,16]{2,1,0:T(4,128)} %bitcast.113), calls=%async_computation.1 | async-start | bytes 65536 | tf_op jit(solution)/shard_map/all_to_all | solution.py:110
  8.2 1.1 %fusion.46 = (f32[6,1,1024]{2,1,0:T(1,128)S(1)}, f32[6,1,1024]{2,1,0:T(1,128)S(1)}) fusion(f32[6,8,1024]{2,1,0:T(8,128)} %param.9), kind=kLoop, calls=%fused_computation.89 | loop fusion | bytes 98304 | tf_op jit(solution)/shard_map/slice | solution.py:16
  9.3 2.3 %collective-permute-start = (f32[6,1,1024]{2,1,0:T(1,128)S(1)}, f32[6,1,1024]{2,1,0:T(1,128)S(1)}, u32[]{:S(2)}, u32[]{:S(2)}) collective-permute-start(f32[6,1,1024]{2,1,0:T(1,128)S(1)} %get-tuple-element.74), channel_id=1, source_target_pairs={{0,1},{1,2},{2,3},{3,4},{4,5},{5,6},{6,7},{7,8},{8,9},{9,10},{10,1... | collective-permute-start | bytes 73736 | tf_op jit(solution)/shard_map/ppermute | solution.py:15
  11.6 1.3 %collective-permute-start.1 = (f32[6,1,1024]{2,1,0:T(1,128)S(1)}, f32[6,1,1024]{2,1,0:T(1,128)S(1)}, u32[]{:S(2)}, u32[]{:S(2)}) collective-permute-start(f32[6,1,1024]{2,1,0:T(1,128)S(1)} %get-tuple-element.75), channel_id=1, source_target_pairs={{1,0},{2,1},{3,2},{4,3},{5,4},{6,5},{7,6},{8,7},{9,8},{10,9},{11,1... | collective-permute-start | bytes 73736 | tf_op jit(solution)/shard_map/ppermute | solution.py:18
  12.9 1.0 reshape_reshape.20
  13.9 0.8 squeeze.43
  14.7 0.7 fusion.42
  15.4 0.5 fusion.4
  16.2 0.8 reshape.189
  17.0 8.0 %all-to-all-start = ((f32[16,1,384]{2,1,0:T(1,128)}), f32[16,1,384]{2,1,0:T(1,128)S(1)}, u32[]{:S(2)}, u32[]{:S(2)}) async-start(f32[16,1,384]{2,1,0:T(1,128)} %reshape.189), calls=%async_computation | async-start | bytes 49152 | tf_op jit(solution)/shard_map/all_to_all | solution.py:121
  25.0 0.1 squeeze.45
  25.1 0.7 fusion.23
  25.8 0.2 fusion.24
  26.0 1.4 %fusion.8 = (f32[8,1024,6]{1,0,2:T(8,128)}, f32[8,1024,6]{1,0,2:T(8,128)}, f32[8,1024,6]{1,0,2:T(8,128)}, f32[8,1024,6]{1,0,2:T(8,128)}) fusion(f32[8,1024,6]{1,0,2:T(8,128)S(1)} %get-tuple-element.73, bf16[4,6,6,8,1024]{4,3,2,1,0:T(8,128)(2,1)S(1)} %copy-done, f32[8,1024,6]{1,0,2:T(8,128)S(1)} %get-tuple-element.72, ...), kind=kLoop, calls=%fused_computation.18 | loop fusion | flops 3342336 | bytes 3932160 | tf_op jit(solution)/shard_map/abij,bij->aij/dot_general | solution.py:85
  27.5 4.1 %all-to-all-done = f32[16,1,384]{2,1,0:T(1,128)S(1)} async-done(((f32[16,1,384]{2,1,0:T(1,128)}), f32[16,1,384]{2,1,0:T(1,128)S(1)}, u32[]{:S(2)}, u32[]{:S(2)}) %all-to-all-start) | async-done | bytes 24608 | tf_op jit(solution)/shard_map/all_to_all | solution.py:121
  31.6 0.5 broadcast.186
  32.1 0.7 reduce.20
  32.8 0.2 reshape.190
  33.0 0.8 mul.150
  33.8 2.7 %fusion.2 = f32[6,64,128]{2,1,0:T(8,128)} fusion(f32[1024,64]{0,1:T(8,128)} %fusion.23, f32[6,1024]{1,0:T(8,128)} %mul.150, s32[1024]{0:T(1024)S(1)} %get-tuple-element.76), kind=kOutput, calls=%fused_computation.2 | convolution fusion | flops 604504064 | bytes 487424 | tf_op jit(solution)/shard_map/while/body/eval_jaxpr/atb,to->abo/dot_general | solution.py:71
  36.5 1.6 %reshape_reshape.22 = f32[6,8,1024]{2,1,0:T(8,128)} reshape(f32[6,64,128]{2,1,0:T(8,128)} %fusion.2) | data formatting | bytes 393216 | tf_op jit(solution)/shard_map/reshape;reshape | solution.py:124
  38.2 2.0 %multiply_reduce_fusion.4 = (f32[]{:T(128)}, f32[8,1024,6]{1,0,2:T(8,128)S(1)}) fusion(f32[6,8,1024]{2,1,0:T(8,128)} %param.8, f32[6,8,1024]{2,1,0:T(8,128)} %reshape_reshape.22, f32[8,1024,6]{1,0,2:T(8,128)} %get-tuple-element.48, f32[8,1024,6]{1,0,2:T(8,128)} %get-tuple-element.49, f32[8,1024,6]{1,0,2:T(8,128)} %get-tuple-element.43, ...), kind=kLoop, calls=%fused_computation.60 | loop fusion | flops 344063 | bytes 1376260 | tf_op jit(solution)/shard_map/reduce_sum | solution.py:114
  40.1 0.1 multiply_reduce_fusion.1
  40.3 0.7 copy-done.2
  40.9 0.6 fusion.45
  41.6 1.6 %reshape_reshape.23 = f32[6,64,128]{2,1,0:T(8,128)} reshape(f32[6,8,1024]{2,1,0:T(8,128)} %bitcast.106) | data formatting | bytes 393216 | tf_op jit(solution)/shard_map/reshape;reshape | solution.py:44
  43.2 2.2 %collective-permute-start.2 = (f32[6,1,1024]{2,1,0:T(1,128)}, f32[6,1,1024]{2,1,0:T(1,128)}, u32[]{:S(2)}, u32[]{:S(2)}) collective-permute-start(f32[6,1,1024]{2,1,0:T(1,128)} %get-tuple-element.68), channel_id=1, source_target_pairs={{0,1},{1,2},{2,3},{3,4},{4,5},{5,6},{6,7},{7,8},{8,9},{9,10},{10,1... | collective-permute-start | bytes 73736 | tf_op jit(solution)/shard_map/ppermute | solution.py:15
  45.4 1.3 %collective-permute-start.3 = (f32[6,1,1024]{2,1,0:T(1,128)}, f32[6,1,1024]{2,1,0:T(1,128)}, u32[]{:S(2)}, u32[]{:S(2)}) collective-permute-start(f32[6,1,1024]{2,1,0:T(1,128)} %get-tuple-element.69), channel_id=1, source_target_pairs={{1,0},{2,1},{3,2},{4,3},{5,4},{6,5},{7,6},{8,7},{9,8},{10,9},{11,1... | collective-permute-start | bytes 73736 | tf_op jit(solution)/shard_map/ppermute | solution.py:18
  46.7 1.5 %fusion.5 = f32[256,6]{0,1:T(8,128)S(1)} fusion(f32[6,64,128]{2,1,0:T(8,128)} %reshape_reshape.23, f32[256,128]{0,1:T(8,128)} %copy-done.13, s32[256]{0:T(256)} %copy-done.16), kind=kOutput, calls=%fused_computation.15 | convolution fusion | flops 151403008 | bytes 334848 | tf_op jit(solution)/shard_map/while/body/eval_jaxpr/tb,abo->tao/dot_general | solution.py:50
  48.3 0.7 reshape_reshape.24
  49.0 0.8 broadcast_multiply_fusion.2
  49.8 1.5 %fusion.48 = f32[16,6,4,16]{3,2,1,0:T(4,128)} fusion(f32[16,4,16]{2,1,0:T(4,128)} %bitcast.111, f32[6,16,16]{2,0,1:T(8,128)S(1)} %copy.14), kind=kLoop, calls=%fused_computation.91 | loop fusion | flops 6144 | bytes 34816
  51.3 1.7 %reshape.191 = f32[16,1,384]{2,1,0:T(1,128)} reshape(f32[16,6,4,16]{3,2,1,0:T(4,128)} %fusion.48) | data formatting | bytes 49152
  53.0 4.9 %all-to-all-start.2 = ((f32[16,1,384]{2,1,0:T(1,128)}), f32[16,1,384]{2,1,0:T(1,128)}, u32[]{:S(2)}, u32[]{:S(2)}) async-start(f32[16,1,384]{2,1,0:T(1,128)} %reshape.191), calls=%async_computation.2 | async-start | bytes 49152 | tf_op jit(solution)/shard_map/all_to_all | solution.py:121
  57.9 1.4 %fusion.27 = (f32[8,1024,6]{1,0,2:T(8,128)S(1)}, f32[8,1024,6]{1,0,2:T(8,128)S(1)}, f32[8,1024,6]{1,0,2:T(8,128)S(1)}, f32[8,1024,6]{1,0,2:T(8,128)S(1)}) fusion(f32[6,8,1024]{2,1,0:T(8,128)} %bitcast.107, f32[6,1,1024]{2,1,0:T(1,128)} %collective-permute-done.2, f32[6,1,1024]{2,1,0:T(1,128)} %collective-permute-done.3), kind=kLoop, calls=%fused_computation.43 | loop fusion | flops 98304 | bytes 1032192
  59.3 1.4 %fusion.9 = (f32[8,1024,6]{1,0,2:T(8,128)}, f32[8,1024,6]{1,0,2:T(8,128)}, f32[8,1024,6]{1,0,2:T(8,128)}, f32[8,1024,6]{1,0,2:T(8,128)}) fusion(f32[8,1024,6]{1,0,2:T(8,128)S(1)} %get-tuple-element.67, bf16[4,6,6,8,1024]{4,3,2,1,0:T(8,128)(2,1)S(1)} %copy-done, f32[8,1024,6]{1,0,2:T(8,128)S(1)} %get-tuple-element.66, ...), kind=kLoop, calls=%fused_computation.19 | loop fusion | flops 3342336 | bytes 3932160 | tf_op jit(solution)/shard_map/abij,bij->aij/dot_general | solution.py:85
  60.8 3.7 %all-to-all-done.2 = f32[16,1,384]{2,1,0:T(1,128)} async-done(((f32[16,1,384]{2,1,0:T(1,128)}), f32[16,1,384]{2,1,0:T(1,128)}, u32[]{:S(2)}, u32[]{:S(2)}) %all-to-all-start.2) | async-done | bytes 24608 | tf_op jit(solution)/shard_map/all_to_all | solution.py:121
  64.5 1.4 %reduce.21 = f32[16,384]{1,0:T(8,128)S(1)} reduce(f32[16,1,384]{2,1,0:T(1,128)} %all-to-all-done.2, f32[]{:T(128)} %broadcast.186), dimensions={1}, to_apply=%all_to_all.11.reduce_sub_computation | reduce | bytes 49156 | tf_op jit(solution)/shard_map/all_to_all | solution.py:121
  66.0 0.2 reshape.192
  66.2 0.2 mul.159
  66.4 1.9 %fusion = f32[6,64,128]{2,1,0:T(8,128)S(1)} fusion(f32[6,1024]{1,0:T(8,128)S(1)} %mul.159, f32[1024,64]{0,1:T(8,128)} %fusion.23, s32[1024]{0:T(1024)S(1)} %copy-done.15), kind=kOutput, calls=%fused_computation | convolution fusion | flops 604504064 | bytes 487424 | tf_op jit(solution)/shard_map/while/body/eval_jaxpr/atb,to->abo/dot_general | solution.py:71
  68.5 0.1 multiply_reduce_fusion
  68.6 0.7 copy-done.3
  69.3 0.1 copy-done.5
  69.4 0.8 multiply_reduce_fusion.3
  70.2 2.0 %pad_maximum_fusion.4 = f32[3]{0:T(128)S(1)} fusion(f32[1]{0:T(128)} %bitcast.49, f32[1]{0:T(128)} %bitcast.48, f32[1]{0:T(128)} %bitcast.47), kind=kLoop, calls=%fused_computation.86 | loop fusion | flops 6 | bytes 24 | tf_op jit(solution)/shard_map/stack | solution.py:130
  72.1 30.1 %psum.7 = f32[3]{0:T(128)S(1)} all-reduce(f32[3]{0:T(128)S(1)} %pad_maximum_fusion.4), channel_id=1, replica_groups=mesh['design'=2,'blk'=16] {'blk'}, use_global_device_ids=true, to_apply=%region_5.6 | all-reduce | flops 3 | bytes 24 | tf_op jit(solution)/shard_map/psum | solution.py:130
  102.3 0.6 divide_sqrt_fusion
  (48 shorter events, 0.5 us)
Async XLA Ops:
  0.6 25.2 %copy-start.4 = (f32[6,8,1024]{2,1,0:T(8,128)S(1)}, f32[6,8,1024]{2,1,0:T(8,128)}, u32[]{:S(2)}) copy-start(f32[6,8,1024]{2,1,0:T(8,128)} %param.9) | copy-start | bytes 589828
  0.6 15.5 %copy-start.12 = (f32[1,16,4,16]{3,2,1,0:T(4,128)S(1)}, f32[1,16,4,16]{3,2,1,0:T(4,128)}, u32[]{:S(2)}) copy-start(f32[1,16,4,16]{3,2,1,0:T(4,128)} %param.14) | copy-start | bytes 12292
  0.7 16.4 %all-to-all-start.1 = ((s32[16,4,16]{2,1,0:T(4,128)}), s32[16,4,16]{2,1,0:T(4,128)S(1)}, u32[]{:S(2)}, u32[]{:S(2)}) async-start(s32[16,4,16]{2,1,0:T(4,128)} %bitcast.113), calls=%async_computation.1 | async-start | bytes 65536 | tf_op jit(solution)/shard_map/all_to_all | solution.py:110
  9.3 16.5 %collective-permute-start = (f32[6,1,1024]{2,1,0:T(1,128)S(1)}, f32[6,1,1024]{2,1,0:T(1,128)S(1)}, u32[]{:S(2)}, u32[]{:S(2)}) collective-permute-start(f32[6,1,1024]{2,1,0:T(1,128)S(1)} %get-tuple-element.74), channel_id=1, source_target_pairs={{0,1},{1,2},{2,3},{3,4},{4,5},{5,6},{6,7},{7,8},{8,9},{9,10},{10,1... | collective-permute-start | bytes 73736 | tf_op jit(solution)/shard_map/ppermute | solution.py:15
  11.6 14.2 %collective-permute-start.1 = (f32[6,1,1024]{2,1,0:T(1,128)S(1)}, f32[6,1,1024]{2,1,0:T(1,128)S(1)}, u32[]{:S(2)}, u32[]{:S(2)}) collective-permute-start(f32[6,1,1024]{2,1,0:T(1,128)S(1)} %get-tuple-element.75), channel_id=1, source_target_pairs={{1,0},{2,1},{3,2},{4,3},{5,4},{6,5},{7,6},{8,7},{9,8},{10,9},{11,1... | collective-permute-start | bytes 73736 | tf_op jit(solution)/shard_map/ppermute | solution.py:18
  14.7 11.4 %copy-start.16 = (s32[256]{0:T(256)}, s32[256]{0:T(256)S(1)}, u32[]{:S(2)}) copy-start(s32[256]{0:T(256)S(1)} %get-tuple-element.57) | copy-start | bytes 3076
  15.4 0.6 copy-start.13
  15.4 10.6 %copy-start = (bf16[4,6,6,8,1024]{4,3,2,1,0:T(8,128)(2,1)S(1)}, bf16[4,6,6,8,1024]{4,3,2,1,0:T(8,128)(2,1)}, u32[]{:S(2)}) copy-start(bf16[4,6,6,8,1024]{4,3,2,1,0:T(8,128)(2,1)} %param.11) | copy-start | bytes 7077892
  17.0 14.5 %all-to-all-start = ((f32[16,1,384]{2,1,0:T(1,128)}), f32[16,1,384]{2,1,0:T(1,128)S(1)}, u32[]{:S(2)}, u32[]{:S(2)}) async-start(f32[16,1,384]{2,1,0:T(1,128)} %reshape.189), calls=%async_computation | async-start | bytes 49152 | tf_op jit(solution)/shard_map/all_to_all | solution.py:121
  25.1 8.7 %copy-start.14 = (s32[1024]{0:T(1024)}, s32[1024]{0:T(1024)S(1)}, u32[]{:S(2)}) copy-start(s32[1024]{0:T(1024)S(1)} %get-tuple-element.76) | copy-start | bytes 12292
  33.8 6.3 %copy-start.1 = (f32[6,6,8,1024]{3,2,1,0:T(8,128)S(1)}, f32[6,6,8,1024]{3,2,1,0:T(8,128)}, u32[]{:S(2)}) copy-start(f32[6,6,8,1024]{3,2,1,0:T(8,128)} %param.10) | copy-start | bytes 3538948
  40.3 0.7 copy-start.2
  43.2 14.7 %collective-permute-start.2 = (f32[6,1,1024]{2,1,0:T(1,128)}, f32[6,1,1024]{2,1,0:T(1,128)}, u32[]{:S(2)}, u32[]{:S(2)}) collective-permute-start(f32[6,1,1024]{2,1,0:T(1,128)} %get-tuple-element.68), channel_id=1, source_target_pairs={{0,1},{1,2},{2,3},{3,4},{4,5},{5,6},{6,7},{7,8},{8,9},{9,10},{10,1... | collective-permute-start | bytes 73736 | tf_op jit(solution)/shard_map/ppermute | solution.py:15
  45.4 12.5 %collective-permute-start.3 = (f32[6,1,1024]{2,1,0:T(1,128)}, f32[6,1,1024]{2,1,0:T(1,128)}, u32[]{:S(2)}, u32[]{:S(2)}) collective-permute-start(f32[6,1,1024]{2,1,0:T(1,128)} %get-tuple-element.69), channel_id=1, source_target_pairs={{1,0},{2,1},{3,2},{4,3},{5,4},{6,5},{7,6},{8,7},{9,8},{10,9},{11,1... | collective-permute-start | bytes 73736 | tf_op jit(solution)/shard_map/ppermute | solution.py:18
  53.0 11.5 %all-to-all-start.2 = ((f32[16,1,384]{2,1,0:T(1,128)}), f32[16,1,384]{2,1,0:T(1,128)}, u32[]{:S(2)}, u32[]{:S(2)}) async-start(f32[16,1,384]{2,1,0:T(1,128)} %reshape.191), calls=%async_computation.2 | async-start | bytes 49152 | tf_op jit(solution)/shard_map/all_to_all | solution.py:121
  59.3 7.0 %copy-start.15 = (s32[1024]{0:T(1024)S(1)}, s32[1024]{0:T(1024)}, u32[]{:S(2)}) copy-start(s32[1024]{0:T(1024)} %copy-done.14) | copy-start | bytes 12292
  60.8 7.6 %copy-start.7 = (f32[6,8,1024]{2,1,0:T(8,128)S(1)}, f32[6,8,1024]{2,1,0:T(8,128)}, u32[]{:S(2)}) copy-start(f32[6,8,1024]{2,1,0:T(8,128)} %param.8) | copy-start | bytes 589828
  60.8 7.6 %copy-start.8 = (f32[8,1024,6]{1,0,2:T(8,128)S(1)}, f32[8,1024,6]{1,0,2:T(8,128)}, u32[]{:S(2)}) copy-start(f32[8,1024,6]{1,0,2:T(8,128)} %get-tuple-element.34) | copy-start | bytes 589828
  60.8 7.6 %copy-start.9 = (f32[8,1024,6]{1,0,2:T(8,128)S(1)}, f32[8,1024,6]{1,0,2:T(8,128)}, u32[]{:S(2)}) copy-start(f32[8,1024,6]{1,0,2:T(8,128)} %get-tuple-element.35) | copy-start | bytes 589828
  60.8 7.6 %copy-start.10 = (f32[8,1024,6]{1,0,2:T(8,128)S(1)}, f32[8,1024,6]{1,0,2:T(8,128)}, u32[]{:S(2)}) copy-start(f32[8,1024,6]{1,0,2:T(8,128)} %get-tuple-element.40) | copy-start | bytes 589828
  60.8 7.6 %copy-start.11 = (f32[8,1024,6]{1,0,2:T(8,128)S(1)}, f32[8,1024,6]{1,0,2:T(8,128)}, u32[]{:S(2)}) copy-start(f32[8,1024,6]{1,0,2:T(8,128)} %get-tuple-element.41) | copy-start | bytes 589828
  68.4 0.9 copy-start.3
  68.4 1.0 copy-start.5
  69.4 33.5 %copy-start.6 = (f32[8,1024,6]{1,0,2:T(8,128)}, f32[8,1024,6]{1,0,2:T(8,128)S(1)}, u32[]{:S(2)}) copy-start(f32[8,1024,6]{1,0,2:T(8,128)S(1)} %multiply_reduce_fusion) | copy-start | bytes 589828
where the time goes:
time: 104 us; the launch traced here: 103 us
  blocking collectives  30.1 us (29%)
  starting transfers between devices  27.5 us (26%)
  other arithmetic  16 us (15%)
  local copies, waits for them, and re-layouts  13.7 us (13%)
  waiting for transfers between devices  7.82 us (8%)
  matrix products  6.72 us (6%)
  between operations  1.06 us (1%)
    psum x1, blocking collectives, body(): totals = lax.psum(jnp.stack([rhs_local] + partials), 'blk')  30.1 us
    all_to_all x2, starting transfers between devices, body(): lax.all_to_all(weighted, 'blk', split_axis=1, concat_axis=1, tiled=True)  12.9 us
    all_to_all x2, waiting for transfers between devices, body(): lax.all_to_all(weighted, 'blk', split_axis=1, concat_axis=1, tiled=True)  7.81 us
    all_to_all x1, starting transfers between devices, body(): lax.all_to_all(donor_cell[0], 'blk', split_axis=0, concat_axis=0, tiled=T...  7.56 us
    dot_general x2, matrix products, spread_one_group(): jnp.einsum('atb,to->abo', weighted, offset_hot, precision=lax.Precision.H...  4.65 us
    ppermute x2, starting transfers between devices, padded_2(): lax.ppermute(lax.slice_in_dim(block, block.shape[dim] - width, None, axis...  4.52 us
    unnamed x38, local copies, waits for them, and re-layouts  4.45 us
    unnamed x5, other arithmetic  3.18 us
  transfers between devices with their start and end apart: 7, of which 2 were waited for; matrix products, arithmetic and copies ran while one was open for 16% of the time, Pallas kernels for 0%

commit v1 on v0

--- a/solution.py
+++ b/solution.py
@@ -127,7 +127,7 @@
         partial_sq = jnp.sum(change * change)
         partials.append(partial_sq)
         psi = new
-    totals = lax.psum(jnp.stack([rhs_local] + partials), "blk")
+    totals = jnp.sum(lax.all_gather(jnp.stack([rhs_local] + partials), "blk"), axis=0)
     result_norms = jnp.sqrt(totals[1:] / (totals[0] + 1e-06))
     return (psi, result_norms)
 

time: 104 us -> 107 us (1.029)
  other arithmetic: 16 us -> 17.1 us
    unnamed x0 -> x1, blocking collectives: none -> 30.1 us
    psum x1 -> x0, blocking collectives: 30.1 us -> none  [body(): totals = lax.psum(jnp.stack([rhs_local] + partials), 'blk')]
    unnamed x5 -> x6, other arithmetic: 3.18 us -> 5.35 us
    another operation x1 -> x0, other arithmetic: 1.95 us -> none  [body(): totals = lax.psum(jnp.stack([rhs_local] + partials), 'blk')]
    unnamed x38 -> x40, local copies, waits for them, and re-layouts: 4.45 us -> 4.35 us
  transfers between devices with their start and end apart: 7 -> 7, of which waited for: 2 -> 2; matrix products, arithmetic and copies ran while one was open for 16% -> 13% of each run, Pallas kernels for 0% -> 0%
where the time goes in v1:
time: 107 us; the launch traced here: 106 us
  blocking collectives  30.1 us (28%)
  starting transfers between devices  27.5 us (26%)
  other arithmetic  17.1 us (16%)
  local copies, waits for them, and re-layouts  14.7 us (14%)
  waiting for transfers between devices  7.83 us (7%)
  matrix products  6.73 us (6%)
  between operations  1.74 us (2%)
    unnamed x1, blocking collectives  30.1 us
    all_to_all x2, starting transfers between devices, body(): lax.all_to_all(weighted, 'blk', split_axis=1, concat_axis=1, tiled=True)  12.9 us
    all_to_all x2, waiting for transfers between devices, body(): lax.all_to_all(weighted, 'blk', split_axis=1, concat_axis=1, tiled=True)  7.82 us
    all_to_all x1, starting transfers between devices, body(): lax.all_to_all(donor_cell[0], 'blk', split_axis=0, concat_axis=0, tiled=T...  7.56 us
    unnamed x6, other arithmetic  5.35 us
    dot_general x2, matrix products, spread_one_group(): jnp.einsum('atb,to->abo', weighted, offset_hot, precision=lax.Precision.H...  4.65 us
    ppermute x2, starting transfers between devices, padded_2(): lax.ppermute(lax.slice_in_dim(block, block.shape[dim] - width, None, axis...  4.53 us
    unnamed x40, local copies, waits for them, and re-layouts  4.35 us
  transfers between devices with their start and end apart: 7, of which 2 were waited for; matrix products, arithmetic and copies ran while one was open for 13% of the time, Pallas kernels for 0%

profile of v1, /device:TPU:0, one launch (start us, length us, event | category | flops | bytes accessed | tf_op | source)
XLA Modules:
  0.0 105.7 jit_solution(4198142137280219755)
XLA Ops:
  0.7 7.6 %all-to-all-start.1 = ((s32[16,4,16]{2,1,0:T(4,128)}), s32[16,4,16]{2,1,0:T(4,128)S(1)}, u32[]{:S(2)}, u32[]{:S(2)}) async-start(s32[16,4,16]{2,1,0:T(4,128)} %bitcast.114), calls=%async_computation.1 | async-start | bytes 65536 | tf_op jit(solution)/shard_map/all_to_all | solution.py:110
  8.2 1.1 %fusion.46 = (f32[6,1,1024]{2,1,0:T(1,128)S(1)}, f32[6,1,1024]{2,1,0:T(1,128)S(1)}) fusion(f32[6,8,1024]{2,1,0:T(8,128)} %param.9), kind=kLoop, calls=%fused_computation.89 | loop fusion | bytes 98304 | tf_op jit(solution)/shard_map/slice | solution.py:16
  9.3 2.3 %collective-permute-start = (f32[6,1,1024]{2,1,0:T(1,128)S(1)}, f32[6,1,1024]{2,1,0:T(1,128)S(1)}, u32[]{:S(2)}, u32[]{:S(2)}) collective-permute-start(f32[6,1,1024]{2,1,0:T(1,128)S(1)} %get-tuple-element.74), channel_id=1, source_target_pairs={{0,1},{1,2},{2,3},{3,4},{4,5},{5,6},{6,7},{7,8},{8,9},{9,10},{10,1... | collective-permute-start | bytes 73736 | tf_op jit(solution)/shard_map/ppermute | solution.py:15
  11.6 1.3 %collective-permute-start.1 = (f32[6,1,1024]{2,1,0:T(1,128)S(1)}, f32[6,1,1024]{2,1,0:T(1,128)S(1)}, u32[]{:S(2)}, u32[]{:S(2)}) collective-permute-start(f32[6,1,1024]{2,1,0:T(1,128)S(1)} %get-tuple-element.75), channel_id=1, source_target_pairs={{1,0},{2,1},{3,2},{4,3},{5,4},{6,5},{7,6},{8,7},{9,8},{10,9},{11,1... | collective-permute-start | bytes 73736 | tf_op jit(solution)/shard_map/ppermute | solution.py:18
  12.9 1.0 reshape_reshape.20
  13.9 0.8 squeeze.43
  14.7 0.5 fusion.4
  15.4 0.8 fusion.42
  16.3 0.8 reshape.195
  17.1 0.6 dynamic-slice
  18.3 8.0 %all-to-all-start = ((f32[16,1,384]{2,1,0:T(1,128)}), f32[16,1,384]{2,1,0:T(1,128)S(1)}, u32[]{:S(2)}, u32[]{:S(2)}) async-start(f32[16,1,384]{2,1,0:T(1,128)} %reshape.195), calls=%async_computation | async-start | bytes 49152 | tf_op jit(solution)/shard_map/all_to_all | solution.py:121
  26.3 0.1 squeeze.45
  26.4 0.7 fusion.23
  27.2 0.2 fusion.24
  27.4 1.4 %fusion.8 = (f32[8,1024,6]{1,0,2:T(8,128)}, f32[8,1024,6]{1,0,2:T(8,128)}, f32[8,1024,6]{1,0,2:T(8,128)}, f32[8,1024,6]{1,0,2:T(8,128)}) fusion(f32[8,1024,6]{1,0,2:T(8,128)S(1)} %get-tuple-element.73, bf16[4,6,6,8,1024]{4,3,2,1,0:T(8,128)(2,1)S(1)} %copy-done, f32[8,1024,6]{1,0,2:T(8,128)S(1)} %get-tuple-element.72, ...), kind=kLoop, calls=%fused_computation.18 | loop fusion | flops 3342336 | bytes 3932160 | tf_op jit(solution)/shard_map/abij,bij->aij/dot_general | solution.py:85
  28.8 4.1 %all-to-all-done = f32[16,1,384]{2,1,0:T(1,128)S(1)} async-done(((f32[16,1,384]{2,1,0:T(1,128)}), f32[16,1,384]{2,1,0:T(1,128)S(1)}, u32[]{:S(2)}, u32[]{:S(2)}) %all-to-all-start) | async-done | bytes 24608 | tf_op jit(solution)/shard_map/all_to_all | solution.py:121
  32.9 0.5 broadcast.187
  33.4 0.7 reduce.20
  34.1 0.2 reshape.196
  34.3 0.8 mul.150
  35.1 2.7 %fusion.2 = f32[6,64,128]{2,1,0:T(8,128)} fusion(f32[1024,64]{0,1:T(8,128)} %fusion.23, f32[6,1024]{1,0:T(8,128)} %mul.150, s32[1024]{0:T(1024)S(1)} %get-tuple-element.76), kind=kOutput, calls=%fused_computation.2 | convolution fusion | flops 604504064 | bytes 487424 | tf_op jit(solution)/shard_map/while/body/eval_jaxpr/atb,to->abo/dot_general | solution.py:71
  37.8 1.6 %reshape_reshape.22 = f32[6,8,1024]{2,1,0:T(8,128)} reshape(f32[6,64,128]{2,1,0:T(8,128)} %fusion.2) | data formatting | bytes 393216 | tf_op jit(solution)/shard_map/reshape;reshape | solution.py:124
  39.5 2.1 %multiply_reduce_fusion.4 = (f32[]{:T(128)}, f32[8,1024,6]{1,0,2:T(8,128)S(1)}) fusion(f32[6,8,1024]{2,1,0:T(8,128)} %param.8, f32[6,8,1024]{2,1,0:T(8,128)} %reshape_reshape.22, f32[8,1024,6]{1,0,2:T(8,128)} %get-tuple-element.48, f32[8,1024,6]{1,0,2:T(8,128)} %get-tuple-element.49, f32[8,1024,6]{1,0,2:T(8,128)} %get-tuple-element.43, ...), kind=kLoop, calls=%fused_computation.60 | loop fusion | flops 344063 | bytes 1376260 | tf_op jit(solution)/shard_map/reduce_sum | solution.py:114
  41.6 0.8 multiply_reduce_fusion.1
  42.3 1.6 %reshape_reshape.23 = f32[6,64,128]{2,1,0:T(8,128)} reshape(f32[6,8,1024]{2,1,0:T(8,128)} %bitcast.106) | data formatting | bytes 393216 | tf_op jit(solution)/shard_map/reshape;reshape | solution.py:44
  44.0 1.7 %fusion.45 = (f32[6,1,1024]{2,1,0:T(1,128)}, f32[6,1,1024]{2,1,0:T(1,128)}) fusion(f32[6,8,1024]{2,1,0:T(8,128)} %bitcast.107), kind=kLoop, calls=%fused_computation.88 | loop fusion | bytes 98304 | tf_op jit(solution)/shard_map/slice | solution.py:16
  45.7 1.5 %fusion.5 = f32[256,6]{0,1:T(8,128)S(1)} fusion(f32[6,64,128]{2,1,0:T(8,128)} %reshape_reshape.23, f32[256,128]{0,1:T(8,128)} %copy-done.12, s32[256]{0:T(256)} %copy-done.15), kind=kOutput, calls=%fused_computation.15 | convolution fusion | flops 151403008 | bytes 334848 | tf_op jit(solution)/shard_map/while/body/eval_jaxpr/tb,abo->tao/dot_general | solution.py:50
  47.2 0.7 reshape_reshape.24
  47.9 0.8 broadcast_multiply_fusion.2
  48.7 2.2 %collective-permute-start.2 = (f32[6,1,1024]{2,1,0:T(1,128)}, f32[6,1,1024]{2,1,0:T(1,128)}, u32[]{:S(2)}, u32[]{:S(2)}) collective-permute-start(f32[6,1,1024]{2,1,0:T(1,128)} %get-tuple-element.68), channel_id=1, source_target_pairs={{0,1},{1,2},{2,3},{3,4},{4,5},{5,6},{6,7},{7,8},{8,9},{9,10},{10,1... | collective-permute-start | bytes 73736 | tf_op jit(solution)/shard_map/ppermute | solution.py:15
  50.9 1.3 %collective-permute-start.3 = (f32[6,1,1024]{2,1,0:T(1,128)}, f32[6,1,1024]{2,1,0:T(1,128)}, u32[]{:S(2)}, u32[]{:S(2)}) collective-permute-start(f32[6,1,1024]{2,1,0:T(1,128)} %get-tuple-element.69), channel_id=1, source_target_pairs={{1,0},{2,1},{3,2},{4,3},{5,4},{6,5},{7,6},{8,7},{9,8},{10,9},{11,1... | collective-permute-start | bytes 73736 | tf_op jit(solution)/shard_map/ppermute | solution.py:18
  52.2 1.5 %fusion.48 = f32[16,6,4,16]{3,2,1,0:T(4,128)} fusion(f32[16,4,16]{2,1,0:T(4,128)} %bitcast.112, f32[6,16,16]{2,0,1:T(8,128)S(1)} %copy.14), kind=kLoop, calls=%fused_computation.91 | loop fusion | flops 6144 | bytes 34816
  53.7 1.7 %reshape.197 = f32[16,1,384]{2,1,0:T(1,128)} reshape(f32[16,6,4,16]{3,2,1,0:T(4,128)} %fusion.48) | data formatting | bytes 49152
  55.4 4.9 %all-to-all-start.2 = ((f32[16,1,384]{2,1,0:T(1,128)}), f32[16,1,384]{2,1,0:T(1,128)}, u32[]{:S(2)}, u32[]{:S(2)}) async-start(f32[16,1,384]{2,1,0:T(1,128)} %reshape.197), calls=%async_computation.2 | async-start | bytes 49152 | tf_op jit(solution)/shard_map/all_to_all | solution.py:121
  60.3 1.4 %fusion.27 = (f32[8,1024,6]{1,0,2:T(8,128)S(1)}, f32[8,1024,6]{1,0,2:T(8,128)S(1)}, f32[8,1024,6]{1,0,2:T(8,128)S(1)}, f32[8,1024,6]{1,0,2:T(8,128)S(1)}) fusion(f32[6,8,1024]{2,1,0:T(8,128)} %bitcast.108, f32[6,1,1024]{2,1,0:T(1,128)} %collective-permute-done.2, f32[6,1,1024]{2,1,0:T(1,128)} %collective-permute-done.3), kind=kLoop, calls=%fused_computation.43 | loop fusion | flops 98304 | bytes 1032192
  61.8 1.4 %fusion.9 = (f32[8,1024,6]{1,0,2:T(8,128)}, f32[8,1024,6]{1,0,2:T(8,128)}, f32[8,1024,6]{1,0,2:T(8,128)}, f32[8,1024,6]{1,0,2:T(8,128)}) fusion(f32[8,1024,6]{1,0,2:T(8,128)S(1)} %get-tuple-element.67, bf16[4,6,6,8,1024]{4,3,2,1,0:T(8,128)(2,1)S(1)} %copy-done, f32[8,1024,6]{1,0,2:T(8,128)S(1)} %get-tuple-element.66, ...), kind=kLoop, calls=%fused_computation.19 | loop fusion | flops 3342336 | bytes 3932160 | tf_op jit(solution)/shard_map/abij,bij->aij/dot_general | solution.py:85
  63.2 3.7 %all-to-all-done.2 = f32[16,1,384]{2,1,0:T(1,128)} async-done(((f32[16,1,384]{2,1,0:T(1,128)}), f32[16,1,384]{2,1,0:T(1,128)}, u32[]{:S(2)}, u32[]{:S(2)}) %all-to-all-start.2) | async-done | bytes 24608 | tf_op jit(solution)/shard_map/all_to_all | solution.py:121
  67.0 1.4 %reduce.21 = f32[16,384]{1,0:T(8,128)S(1)} reduce(f32[16,1,384]{2,1,0:T(1,128)} %all-to-all-done.2, f32[]{:T(128)} %broadcast.187), dimensions={1}, to_apply=%all_to_all.11.reduce_sub_computation | reduce | bytes 49156 | tf_op jit(solution)/shard_map/all_to_all | solution.py:121
  68.4 0.2 reshape.198
  68.6 0.2 mul.159
  68.8 1.9 %fusion = f32[6,64,128]{2,1,0:T(8,128)S(1)} fusion(f32[6,1024]{1,0:T(8,128)S(1)} %mul.159, f32[1024,64]{0,1:T(8,128)} %fusion.23, s32[1024]{0:T(1024)S(1)} %copy-done.14), kind=kOutput, calls=%fused_computation | convolution fusion | flops 604504064 | bytes 487424 | tf_op jit(solution)/shard_map/while/body/eval_jaxpr/atb,to->abo/dot_general | solution.py:71
  70.9 0.1 multiply_reduce_fusion
  71.1 0.7 copy-done.2
  71.8 0.1 copy-done.4
  71.9 0.8 multiply_reduce_fusion.3
  72.6 2.2 %maximum_dynamic-update-slice_fusion = f32[48]{0:T(128)S(1)} fusion(f32[48]{0:T(128)S(1)} %broadcast.166, u32[]{:T(128)} %bitcast.50, f32[1]{0:T(128)} %bitcast.49, f32[1]{0:T(128)} %bitcast.48, f32[1]{0:T(128)} %bitcast.47), kind=kLoop, calls=%fused_computation.86 | loop fusion | flops 6 | bytes 208
  74.8 30.1 %all-reduce.2 = f32[48]{0:T(128)S(1)} all-reduce(f32[48]{0:T(128)S(1)} %maximum_dynamic-update-slice_fusion), channel_id=2, replica_groups=mesh['design'=2,'blk'=16] {'blk'}, use_global_device_ids=true, to_apply=%add.2 | all-reduce | flops 48 | bytes 384
  105.1 0.6 divide_sqrt_fusion
  (52 shorter events, 0.6 us)
Async XLA Ops:
  0.6 16.5 %copy-start.16 = (u32[32]{0:T(128)S(1)}, u32[32]{0:T(128)}, u32[]{:S(2)}) copy-start(u32[32]{0:T(128)} %constant.96) | copy-start | bytes 388
  0.6 26.5 %copy-start.3 = (f32[6,8,1024]{2,1,0:T(8,128)S(1)}, f32[6,8,1024]{2,1,0:T(8,128)}, u32[]{:S(2)}) copy-start(f32[6,8,1024]{2,1,0:T(8,128)} %param.9) | copy-start | bytes 589828
  0.7 15.6 %copy-start.11 = (f32[1,16,4,16]{3,2,1,0:T(4,128)S(1)}, f32[1,16,4,16]{3,2,1,0:T(4,128)}, u32[]{:S(2)}) copy-start(f32[1,16,4,16]{3,2,1,0:T(4,128)} %param.14) | copy-start | bytes 12292
  0.7 17.7 %all-to-all-start.1 = ((s32[16,4,16]{2,1,0:T(4,128)}), s32[16,4,16]{2,1,0:T(4,128)S(1)}, u32[]{:S(2)}, u32[]{:S(2)}) async-start(s32[16,4,16]{2,1,0:T(4,128)} %bitcast.114), calls=%async_computation.1 | async-start | bytes 65536 | tf_op jit(solution)/shard_map/all_to_all | solution.py:110
  9.3 17.9 %collective-permute-start = (f32[6,1,1024]{2,1,0:T(1,128)S(1)}, f32[6,1,1024]{2,1,0:T(1,128)S(1)}, u32[]{:S(2)}, u32[]{:S(2)}) collective-permute-start(f32[6,1,1024]{2,1,0:T(1,128)S(1)} %get-tuple-element.74), channel_id=1, source_target_pairs={{0,1},{1,2},{2,3},{3,4},{4,5},{5,6},{6,7},{7,8},{8,9},{9,10},{10,1... | collective-permute-start | bytes 73736 | tf_op jit(solution)/shard_map/ppermute | solution.py:15
  11.6 15.5 %collective-permute-start.1 = (f32[6,1,1024]{2,1,0:T(1,128)S(1)}, f32[6,1,1024]{2,1,0:T(1,128)S(1)}, u32[]{:S(2)}, u32[]{:S(2)}) collective-permute-start(f32[6,1,1024]{2,1,0:T(1,128)S(1)} %get-tuple-element.75), channel_id=1, source_target_pairs={{1,0},{2,1},{3,2},{4,3},{5,4},{6,5},{7,6},{8,7},{9,8},{10,9},{11,1... | collective-permute-start | bytes 73736 | tf_op jit(solution)/shard_map/ppermute | solution.py:18
  14.7 0.6 copy-start.15
  14.7 0.6 copy-start.12
  14.7 12.6 %copy-start = (bf16[4,6,6,8,1024]{4,3,2,1,0:T(8,128)(2,1)S(1)}, bf16[4,6,6,8,1024]{4,3,2,1,0:T(8,128)(2,1)}, u32[]{:S(2)}) copy-start(bf16[4,6,6,8,1024]{4,3,2,1,0:T(8,128)(2,1)} %param.11) | copy-start | bytes 7077892
  18.3 14.6 %all-to-all-start = ((f32[16,1,384]{2,1,0:T(1,128)}), f32[16,1,384]{2,1,0:T(1,128)S(1)}, u32[]{:S(2)}, u32[]{:S(2)}) async-start(f32[16,1,384]{2,1,0:T(1,128)} %reshape.195), calls=%async_computation | async-start | bytes 49152 | tf_op jit(solution)/shard_map/all_to_all | solution.py:121
  26.4 8.7 %copy-start.13 = (s32[1024]{0:T(1024)}, s32[1024]{0:T(1024)S(1)}, u32[]{:S(2)}) copy-start(s32[1024]{0:T(1024)S(1)} %get-tuple-element.76) | copy-start | bytes 12292
  35.1 6.4 %copy-start.1 = (f32[6,6,8,1024]{3,2,1,0:T(8,128)S(1)}, f32[6,6,8,1024]{3,2,1,0:T(8,128)}, u32[]{:S(2)}) copy-start(f32[6,6,8,1024]{3,2,1,0:T(8,128)} %param.10) | copy-start | bytes 3538948
  48.7 11.6 %collective-permute-start.2 = (f32[6,1,1024]{2,1,0:T(1,128)}, f32[6,1,1024]{2,1,0:T(1,128)}, u32[]{:S(2)}, u32[]{:S(2)}) collective-permute-start(f32[6,1,1024]{2,1,0:T(1,128)} %get-tuple-element.68), channel_id=1, source_target_pairs={{0,1},{1,2},{2,3},{3,4},{4,5},{5,6},{6,7},{7,8},{8,9},{9,10},{10,1... | collective-permute-start | bytes 73736 | tf_op jit(solution)/shard_map/ppermute | solution.py:15
  50.9 9.4 %collective-permute-start.3 = (f32[6,1,1024]{2,1,0:T(1,128)}, f32[6,1,1024]{2,1,0:T(1,128)}, u32[]{:S(2)}, u32[]{:S(2)}) collective-permute-start(f32[6,1,1024]{2,1,0:T(1,128)} %get-tuple-element.69), channel_id=1, source_target_pairs={{1,0},{2,1},{3,2},{4,3},{5,4},{6,5},{7,6},{8,7},{9,8},{10,9},{11,1... | collective-permute-start | bytes 73736 | tf_op jit(solution)/shard_map/ppermute | solution.py:18
  55.4 11.5 %all-to-all-start.2 = ((f32[16,1,384]{2,1,0:T(1,128)}), f32[16,1,384]{2,1,0:T(1,128)}, u32[]{:S(2)}, u32[]{:S(2)}) async-start(f32[16,1,384]{2,1,0:T(1,128)} %reshape.197), calls=%async_computation.2 | async-start | bytes 49152 | tf_op jit(solution)/shard_map/all_to_all | solution.py:121
  61.8 7.0 %copy-start.14 = (s32[1024]{0:T(1024)S(1)}, s32[1024]{0:T(1024)}, u32[]{:S(2)}) copy-start(s32[1024]{0:T(1024)} %copy-done.13) | copy-start | bytes 12292
  63.2 7.6 %copy-start.6 = (f32[6,8,1024]{2,1,0:T(8,128)S(1)}, f32[6,8,1024]{2,1,0:T(8,128)}, u32[]{:S(2)}) copy-start(f32[6,8,1024]{2,1,0:T(8,128)} %param.8) | copy-start | bytes 589828
  63.2 7.6 %copy-start.7 = (f32[8,1024,6]{1,0,2:T(8,128)S(1)}, f32[8,1024,6]{1,0,2:T(8,128)}, u32[]{:S(2)}) copy-start(f32[8,1024,6]{1,0,2:T(8,128)} %get-tuple-element.34) | copy-start | bytes 589828
  63.2 7.6 %copy-start.8 = (f32[8,1024,6]{1,0,2:T(8,128)S(1)}, f32[8,1024,6]{1,0,2:T(8,128)}, u32[]{:S(2)}) copy-start(f32[8,1024,6]{1,0,2:T(8,128)} %get-tuple-element.35) | copy-start | bytes 589828
  63.2 7.6 %copy-start.9 = (f32[8,1024,6]{1,0,2:T(8,128)S(1)}, f32[8,1024,6]{1,0,2:T(8,128)}, u32[]{:S(2)}) copy-start(f32[8,1024,6]{1,0,2:T(8,128)} %get-tuple-element.40) | copy-start | bytes 589828
  63.2 7.6 %copy-start.10 = (f32[8,1024,6]{1,0,2:T(8,128)S(1)}, f32[8,1024,6]{1,0,2:T(8,128)}, u32[]{:S(2)}) copy-start(f32[8,1024,6]{1,0,2:T(8,128)} %get-tuple-element.41) | copy-start | bytes 589828
  70.8 0.9 copy-start.2
  70.9 1.0 copy-start.4
  71.9 33.8 %copy-start.5 = (f32[8,1024,6]{1,0,2:T(8,128)}, f32[8,1024,6]{1,0,2:T(8,128)S(1)}, u32[]{:S(2)}) copy-start(f32[8,1024,6]{1,0,2:T(8,128)S(1)} %multiply_reduce_fusion) | copy-start | bytes 589828
